TPU v7x, 32 devices: a whole 2x2x4 slice. The times are simulated.
32 devices in a mesh: walker: 2 (over x), owner: 4 (over y, core), replica: 4 (over z).
Axes of the slice: x: 2, y: 2, z: 4, core: 2. Of those that a mesh axis runs over, the one named last changes fastest.
Arguments:
- layer_inputs: bfloat16 [4, 61440, 832], P(None, ('walker', 'owner', 'replica')), may hold values from -6 to 6
- layer_grads: bfloat16 [4, 61440, 256], P(None, ('walker', 'owner', 'replica')), may hold values from -6 to 6
- local_energy: float32 [1024], P(('walker', 'owner', 'replica')), may hold values from -3 to 1
Outputs:
- step: float32 [4, 832, 256], replicated
All inputs are finite; a program needn't handle non-finite values.
Results may differ from a plain program's by a relative error of at most 0.003.
Values sent between devices are 32-bit elements; how exact they have to be, the bound alone decides.
No kernel may reach another device: no remote copies, remote signals or barrier semaphores. Data moves between devices by JAX's collectives and lax.ppermute only.
A program may use at most 128 MiB of HBM per device.

v0:
```python
import jax
import jax.numpy as jnp
from jax import lax
from jax.sharding import PartitionSpec as P


def shards(layer_inputs, layer_grads, local_energy):
    walk_count = lax.axis_size("walker")
    owner_count = lax.axis_size("owner")
    replica_count = lax.axis_size("replica")
    devices = walk_count * owner_count * replica_count
    per_walker = local_energy.shape[0]
    walkers = per_walker * devices
    layers, rows, width_in = layer_inputs.shape
    width_out = layer_grads.shape[2]
    all_rows = rows * devices
    total = lax.psum(jnp.sum(local_energy), ("walker", "owner", "replica"))
    centered = local_energy - total / walkers
    weighted = (
        (
            layer_grads.astype(jnp.float32).reshape(
                layers, per_walker, rows // per_walker, width_out
            )
            * centered[None, :, None, None]
        )
        .astype(jnp.bfloat16)
        .reshape(layers, rows, width_out)
    )
    dims = (((1,), (1,)), ((0,), (0,)))
    input_sums = lax.dot_general(
        layer_inputs, layer_inputs, dims, preferred_element_type=jnp.float32
    )
    output_sums = lax.dot_general(
        layer_grads, layer_grads, dims, preferred_element_type=jnp.float32
    )
    grad_sums = lax.dot_general(layer_inputs, weighted, dims, preferred_element_type=jnp.float32)
    sliced = (
        lax.psum_scatter(input_sums, "owner", scatter_dimension=0, tiled=True),
        lax.psum_scatter(output_sums, "owner", scatter_dimension=0, tiled=True),
        lax.psum_scatter(grad_sums, "owner", scatter_dimension=0, tiled=True),
    )
    own_input, own_output, own_grad = lax.psum(
        (sliced[0][0], sliced[1][0], sliced[2][0]), ("walker", "replica")
    )
    ain = own_input / all_rows + 0.1 * jnp.eye(width_in, dtype=jnp.float32)
    gout = own_output / all_rows + 0.1 * jnp.eye(width_out, dtype=jnp.float32)
    grad = own_grad * (2.0 / walkers)
    chol_in = jnp.linalg.cholesky(ain)
    chol_out = jnp.linalg.cholesky(gout)
    left = jax.scipy.linalg.cho_solve((chol_in, True), grad)
    precond = jax.scipy.linalg.cho_solve((chol_out, True), left.T).T
    partial_align = jnp.sum(precond * grad).reshape(1)
    gathered, aligns = (
        lax.all_gather(precond[None], "owner", axis=0, tiled=True),
        lax.all_gather(partial_align, "owner", axis=0, tiled=True),
    )
    return gathered * jnp.sqrt(layers * width_in * width_out / jnp.sum(aligns))


def solution(mesh):
    in_specs = (
        P(None, ("walker", "owner", "replica"), None),
        P(None, ("walker", "owner", "replica"), None),
        P(("walker", "owner", "replica")),
    )
    out_specs = P()
    return jax.shard_map(shards, mesh=mesh, in_specs=in_specs, out_specs=out_specs, check_vma=False)
```

profile of v0, /device:TPU:0, one launch (start us, length us, event | category | flops | bytes accessed | tf_op | source)
XLA Modules:
  0.0 751.3 jit_solution(12996751452500109084)
XLA Ops:
  6.5 5.8 fusion.103
  13.1 42.2 %psum.30 = f32[]{:T(128)} all-reduce(f32[]{:T(128)} %reduce_sum.27), channel_id=1, replica_groups=mesh['walker'=2,'owner'=4,'replica'=4] {'walker','owner','replica'}, use_global_device_ids=true, to_apply=%region_23.24 | all-reduce | flops 1 | bytes 8 | tf_op jit(solution)/shard_map/psum | solution.py:17
  56.1 11.3 %fusion.3 = f32[4,832,256]{2,1,0:T(8,128)} fusion(bf16[4,1920,832]{1,2,0:T(8,128)(2,1)} %param.3, bf16[4,1920,256]{2,1,0:T(8,128)(2,1)} %param.4, f32[1920]{0:T(1024)S(1)} %mul.45), kind=kOutput, calls=%fused_computation.13 | convolution fusion | flops 3277455360 | bytes 20127232 | tf_op jit(solution)/shard_map/dot_general | solution.py:36
  67.4 25.0 %fusion.104 = f32[4,832,832]{2,1,0:T(8,128)} fusion(bf16[4,1920,832]{1,2,0:T(8,128)(2,1)} %param.3), kind=kOutput, calls=%fused_computation.232 | convolution fusion | flops 10632560640 | bytes 23855104 | tf_op jit(solution)/shard_map/dot_general | solution.py:30
  92.5 14.5 %reduce-scatter.8.cloned.1.call-done = f32[1,832,256]{2,1,0:T(8,128)} async-done(((f32[4,832,256]{2,1,0:T(8,128)}), f32[1,832,256]{2,1,0:T(8,128)}) %reduce-scatter.8.cloned.1.call-update) | async-done | bytes 851984 | tf_op jit(solution)/shard_map/reduce_scatter | solution.py:40
  107.0 97.9 %reduce-scatter.6.cloned.1.call-done = f32[1,832,832]{2,1,0:T(8,128)} async-done(((f32[4,832,832]{2,1,0:T(8,128)}), f32[1,832,832]{2,1,0:T(8,128)}) %reduce-scatter.6.cloned.1.call-update) | async-done | bytes 2768912 | tf_op jit(solution)/shard_map/reduce_scatter | solution.py:38
  205.7 157.1 %all-reduce.8.cloned.1.call-done = (f32[832,256]{1,0:T(8,128)}, f32[832,832]{1,0:T(8,128)}, f32[256,256]{0,1:T(8,128)}) async-done(((f32[832,256]{1,0:T(8,128)}, f32[832,832]{1,0:T(8,128)}, f32[256,256]{0,1:T(8,128)}), (f32[832,256]{1,0:T(8,128)}, f32[832,832]{1,0:T(8,128)}, f32[256,256]{0,1:T(8,128)})) %all-reduce.8.cloned.1.call-update) | async-done | bytes 3883024 | tf_op jit(solution)/shard_map/psum | solution.py:42
  362.8 3.7 select_add_fusion
  366.5 4.5 copy.11
  374.9 11.7 %cholesky.273 = f32[128,128]{1,0:T(8,128)S(1)} custom-call(f32[128,128]{1,0:T(8,128)S(1)} %cholesky.614), custom_call_target="Cholesky" | custom-call | tf_op jit(solution)/shard_map/jit(cholesky)/cholesky | solution.py:48
  390.1 11.7 %cholesky.237 = f32[128,128]{1,0:T(8,128)S(1)} custom-call(f32[128,128]{1,0:T(8,128)S(1)} %cholesky.611), custom_call_target="Cholesky" | custom-call | tf_op jit(solution)/shard_map/jit(cholesky)/cholesky | solution.py:49
  401.8 9.8 %custom-call.76 = f32[1,128,128]{1,2,0:T(8,128)S(1)} custom-call(f32[1,128,128]{2,1,0:T(8,128)S(1)} %get-tuple-element.59), custom_call_target="InvertDiagBlocksLowerTriangular" | custom-call | tf_op jit(solution)/shard_map/jit(cholesky)/cholesky | solution.py:49
  413.8 11.9 %cholesky.256 = f32[128,128]{1,0:T(8,128)S(1)} custom-call(f32[128,128]{1,0:T(8,128)S(1)} %convolution_subtract_fusion.19), custom_call_target="Cholesky" | custom-call | tf_op jit(solution)/shard_map/jit(cholesky)/cholesky | solution.py:49
  427.3 10.7 %custom-call.78 = f32[1,128,128]{1,2,0:T(8,128)S(1)} custom-call(f32[1,128,128]{2,1,0:T(8,128)} %get-tuple-element.76), custom_call_target="InvertDiagBlocksLowerTriangular" | custom-call | tf_op jit(solution)/shard_map/jit(cholesky)/cholesky | solution.py:48
  441.4 12.5 %cholesky.496 = f32[128,128]{1,0:T(8,128)S(1)} custom-call(f32[128,128]{1,0:T(8,128)} %cholesky.618), custom_call_target="Cholesky" | custom-call | tf_op jit(solution)/shard_map/jit(cholesky)/cholesky | solution.py:48
  454.6 10.6 %custom-call.79 = f32[1,128,128]{1,2,0:T(8,128)S(1)} custom-call(f32[1,128,128]{2,1,0:T(8,128)} %get-tuple-element.73), custom_call_target="InvertDiagBlocksLowerTriangular" | custom-call | tf_op jit(solution)/shard_map/jit(cholesky)/cholesky | solution.py:48
  467.7 11.7 %cholesky.517 = f32[128,128]{1,0:T(8,128)S(1)} custom-call(f32[128,128]{1,0:T(8,128)S(1)} %cholesky.623), custom_call_target="Cholesky" | custom-call | tf_op jit(solution)/shard_map/jit(cholesky)/cholesky | solution.py:48
  480.1 9.8 %custom-call.80 = f32[1,128,128]{1,2,0:T(8,128)S(1)} custom-call(f32[1,128,128]{2,1,0:T(8,128)S(1)} %get-tuple-element.70), custom_call_target="InvertDiagBlocksLowerTriangular" | custom-call | tf_op jit(solution)/shard_map/jit(cholesky)/cholesky | solution.py:48
  491.9 11.7 %cholesky.536 = f32[128,128]{1,0:T(8,128)S(1)} custom-call(f32[128,128]{1,0:T(8,128)S(1)} %cholesky.628), custom_call_target="Cholesky" | custom-call | tf_op jit(solution)/shard_map/jit(cholesky)/cholesky | solution.py:48
  504.3 9.9 %custom-call.81 = f32[1,128,128]{1,2,0:T(8,128)S(1)} custom-call(f32[1,128,128]{2,1,0:T(8,128)S(1)} %get-tuple-element.67), custom_call_target="InvertDiagBlocksLowerTriangular" | custom-call | tf_op jit(solution)/shard_map/jit(cholesky)/cholesky | solution.py:48
  516.2 11.7 %cholesky.555 = f32[128,128]{1,0:T(8,128)S(1)} custom-call(f32[128,128]{1,0:T(8,128)S(1)} %cholesky.633), custom_call_target="Cholesky" | custom-call | tf_op jit(solution)/shard_map/jit(cholesky)/cholesky | solution.py:48
  528.6 9.8 %custom-call.82 = f32[1,128,128]{1,2,0:T(8,128)S(1)} custom-call(f32[1,128,128]{2,1,0:T(8,128)S(1)} %get-tuple-element.64), custom_call_target="InvertDiagBlocksLowerTriangular" | custom-call | tf_op jit(solution)/shard_map/jit(cholesky)/cholesky | solution.py:48
  540.1 11.9 %cholesky.575 = f32[128,128]{1,0:T(8,128)S(1)} custom-call(f32[128,128]{1,0:T(8,128)S(1)} %cholesky.638), custom_call_target="Cholesky" | custom-call | tf_op jit(solution)/shard_map/jit(cholesky)/cholesky | solution.py:48
  552.7 9.8 %custom-call.83 = f32[1,128,128]{1,2,0:T(8,128)S(1)} custom-call(f32[1,128,128]{2,1,0:T(8,128)S(1)} %get-tuple-element.61), custom_call_target="InvertDiagBlocksLowerTriangular" | custom-call | tf_op jit(solution)/shard_map/jit(cholesky)/cholesky | solution.py:48
  563.8 5.8 cholesky.596
  577.3 17.0 %while.3 = (s32[]{:T(128)}, f32[832,832]{1,0:T(8,128)}, s32[6,2]{0,1:T(2,128)S(1)}, f32[6,128,128]{2,1,0:T(8,128)S(1)}, s32[]{:T(128)}) while((s32[]{:T(128)}, f32[832,832]{1,0:T(8,128)}, s32[6,2]{0,1:T(2,128)S(1)}, f32[6,128,128]{2,1,0:T(8,128)S(1)}, s32[]{:T(128)}) %tuple.81), condition=%wide.while_cond.1, body=%wide.while_body.1.sunk | while | flops 2 | bytes 131181 | solution.py:50
  595.2 70.0 %custom-call.84 = f32[7,128,128]{1,2,0:T(8,128)S(1)} custom-call(f32[7,128,128]{2,1,0:T(8,128)} %pad_maximum_fusion), custom_call_target="InvertDiagBlocksLowerTriangular" | custom-call | tf_op jit(solution)/shard_map/jit(_cho_solve)/triangular_solve | solution.py:50
  680.3 5.5 while.2
  685.8 20.8 %custom-call.77 = f32[2,128,128]{1,2,0:T(8,128)S(1)} custom-call(f32[2,128,128]{2,1,0:T(8,128)} %get-tuple-element.12), custom_call_target="InvertDiagBlocksLowerTriangular" | custom-call | tf_op jit(solution)/shard_map/jit(_cho_solve)/triangular_solve | solution.py:51
  714.0 6.4 all-reduce.4
  721.6 18.8 %all-gather.3.cloned.1.call-done = f32[3328,256]{1,0:T(8,128)} async-done(((f32[832,256]{1,0:T(8,128)}), f32[3328,256]{1,0:T(8,128)}) %all-gather.3.cloned.1.call-update) | async-done | bytes 3407888 | tf_op jit(solution)/shard_map/all_gather | solution.py:54
  740.3 3.9 broadcast_multiply_fusion
  (180 shorter events, 76.7 us)
Async XLA Ops:
  6.5 5.9 copy-start.9
  6.5 86.0 %reduce-scatter.4.cloned.1.call-start = ((), (), s32[]{:S(2)}) async-start(), calls=%async_computation.3 | async-start | bytes 1310720 | tf_op jit(solution)/shard_map/reduce_scatter | solution.py:39
  12.4 94.6 %reduce-scatter.8.cloned.1.call-start = ((), (), s32[]{:S(2)}) async-start(), calls=%async_computation.5 | async-start | bytes 4259840 | tf_op jit(solution)/shard_map/reduce_scatter | solution.py:40
  67.3 137.6 %reduce-scatter.6.cloned.1.call-start = ((), (), s32[]{:S(2)}) async-start(), calls=%async_computation.4 | async-start | bytes 14909440 | tf_op jit(solution)/shard_map/reduce_scatter | solution.py:38
  92.5 270.3 %all-reduce.8.cloned.1.call-start = ((), (), s32[]{:S(2)}) async-start(), calls=%async_computation.7 | async-start | bytes 8192000 | tf_op jit(solution)/shard_map/psum | solution.py:42
  205.0 535.3 %all-gather.3.cloned.1.call-start = ((), (), s32[]{:S(2)}) async-start(), calls=%async_computation.6 | async-start | bytes 4259840 | tf_op jit(solution)/shard_map/all_gather | solution.py:54
  366.5 4.5 copy-start
  373.3 1.6 copy-start.3
  374.9 12.6 %copy-start.5 = (f32[256,256]{0,1:T(8,128)S(1)}, f32[256,256]{0,1:T(8,128)}, u32[]{:S(2)}) copy-start(f32[256,256]{0,1:T(8,128)} %get-tuple-element.43) | copy-start | bytes 786436
  389.4 0.7 copy-start.6
  575.4 1.9 copy-start.7
  575.4 18.8 %copy-start.8 = (f32[128,64]{1,0:T(8,128)S(1)}, f32[128,64]{1,0:T(8,128)}, u32[]{:S(2)}) copy-start(f32[128,64]{1,0:T(8,128)} %pad_convert_fusion) | copy-start | bytes 98308
  575.7 1.6 copy-start.1
  594.2 72.4 %copy-start.2 = (f32[832,832]{1,0:T(8,128)S(1)}, f32[832,832]{1,0:T(8,128)}, u32[]{:S(2)}) copy-start(f32[832,832]{1,0:T(8,128)} %get-tuple-element.198) | copy-start | bytes 8306692
  708.2 2.9 copy-start.10
  708.2 3.5 copy-start.4
Sparse Core Ops, SparseCore 0:
  12.5 27.5 reduce-scatter.3
  67.5 39.5 reduce-scatter.7
  109.7 95.2 reduce-scatter.5
  208.8 153.9 all-reduce.7
  711.2 29.0 all-gather.2
where the time goes:
time: 760 us; the launch traced here: 751 us
  waiting for transfers between devices  288 us (38%)
  other arithmetic  285 us (38%)
  matrix products  69.5 us (9%)
  blocking collectives  48.5 us (6%)
  local copies, waits for them, and re-layouts  38.2 us (5%)
  between operations  21.5 us (3%)
    psum x1, waiting for transfers between devices, shards(): lax.psum((sliced[0][0], sliced[1][0], sliced[2][0]), ('walker', 'replica'))  157 us
    another operation x26, other arithmetic, shards(): chol_in = jnp.linalg.cholesky(ain)  143 us
    reduce_scatter x1, waiting for transfers between devices, shards(): lax.psum_scatter(input_sums, 'owner', scatter_dimension=0, tiled=True)  97.9 us
    another operation x7, other arithmetic, shards(): left = jax.scipy.linalg.cho_solve((chol_in, True), grad)  71.7 us
    psum x1, blocking collectives, shards(): total = lax.psum(jnp.sum(local_energy), ('walker', 'owner', 'replica'))  42.2 us
    another operation x6, other arithmetic, shards(): chol_out = jnp.linalg.cholesky(gout)  34.2 us
    dot_general x1, matrix products, shards(): lax.dot_general(layer_inputs, layer_inputs, dims, preferred_element_type=...  25 us
    another operation x28, local copies, waits for them, and re-layouts  22.3 us
  transfers between devices with their start and end apart: 5, of which 4 were waited for; matrix products, arithmetic and copies ran while one was open for 5% of the time, Pallas kernels for 0%

commit v1 on v0

--- a/solution.py
+++ b/solution.py
@@ -40,7 +40,7 @@
         lax.psum_scatter(grad_sums, "owner", scatter_dimension=0, tiled=True),
     )
     own_input, own_output, own_grad = lax.psum(
-        (sliced[0][0], sliced[1][0], sliced[2][0]), ("walker", "replica")
+        lax.psum((sliced[0][0], sliced[1][0], sliced[2][0]), "replica"), "walker"
     )
     ain = own_input / all_rows + 0.1 * jnp.eye(width_in, dtype=jnp.float32)
     gout = own_output / all_rows + 0.1 * jnp.eye(width_out, dtype=jnp.float32)

time: 760 us -> 870 us (1.14)
  waiting for transfers between devices: 288 us -> 393 us
    psum x1 -> x2, waiting for transfers between devices: 157 us -> 261 us  [the longest x1 154 us: shards(): lax.psum((sliced[0][0], sliced[1][0], sliced[2][0]), 'replica')]
  transfers between devices with their start and end apart: 5 -> 6, of which waited for: 4 -> 5; matrix products, arithmetic and copies ran while one was open for 5% -> 5% of each run, Pallas kernels for 0% -> 0%
where the time goes in v1:
time: 870 us; the launch traced here: 862 us
  waiting for transfers between devices  393 us (45%)
  other arithmetic  284 us (33%)
  matrix products  71.9 us (8%)
  blocking collectives  48.5 us (6%)
  local copies, waits for them, and re-layouts  41.9 us (5%)
  between operations  21.9 us (3%)
    psum x1, waiting for transfers between devices, shards(): lax.psum((sliced[0][0], sliced[1][0], sliced[2][0]), 'replica')  154 us
    another operation x26, other arithmetic, shards(): chol_in = jnp.linalg.cholesky(ain)  140 us
    psum x1, waiting for transfers between devices, shards(): lax.psum(lax.psum((sliced[0][0], sliced[1][0], sliced[2][0]), 'replica'),...  106 us
    reduce_scatter x1, waiting for transfers between devices, shards(): lax.psum_scatter(input_sums, 'owner', scatter_dimension=0, tiled=True)  97.9 us
    another operation x7, other arithmetic, shards(): left = jax.scipy.linalg.cho_solve((chol_in, True), grad)  73.3 us
    psum x1, blocking collectives, shards(): total = lax.psum(jnp.sum(local_energy), ('walker', 'owner', 'replica'))  42.2 us
    another operation x6, other arithmetic, shards(): chol_out = jnp.linalg.cholesky(gout)  34 us
    another operation x28, local copies, waits for them, and re-layouts  26.9 us
  transfers between devices with their start and end apart: 6, of which 5 were waited for; matrix products, arithmetic and copies ran while one was open for 5% of the time, Pallas kernels for 0%

profile of v1, /device:TPU:0, one launch (start us, length us, event | category | flops | bytes accessed | tf_op | source)
XLA Modules:
  0.0 861.6 jit_solution(14161724656921550291)
XLA Ops:
  6.5 5.8 fusion.103
  13.1 42.2 %psum.53 = f32[]{:T(128)} all-reduce(f32[]{:T(128)} %reduce_sum.27), channel_id=1, replica_groups=mesh['walker'=2,'owner'=4,'replica'=4] {'walker','owner','replica'}, use_global_device_ids=true, to_apply=%region_25.26 | all-reduce | flops 1 | bytes 8 | tf_op jit(solution)/shard_map/psum | solution.py:17
  56.1 11.3 %fusion.3 = f32[4,832,256]{2,1,0:T(8,128)} fusion(bf16[4,1920,832]{1,2,0:T(8,128)(2,1)} %param.3, bf16[4,1920,256]{2,1,0:T(8,128)(2,1)} %param.4, f32[1920]{0:T(1024)S(1)} %mul.45), kind=kOutput, calls=%fused_computation.13 | convolution fusion | flops 3277455360 | bytes 20127232 | tf_op jit(solution)/shard_map/dot_general | solution.py:36
  67.4 25.0 %fusion.104 = f32[4,832,832]{2,1,0:T(8,128)} fusion(bf16[4,1920,832]{1,2,0:T(8,128)(2,1)} %param.3), kind=kOutput, calls=%fused_computation.232 | convolution fusion | flops 10632560640 | bytes 23855104 | tf_op jit(solution)/shard_map/dot_general | solution.py:30
  92.5 14.5 %reduce-scatter.8.cloned.1.call-done = f32[1,832,256]{2,1,0:T(8,128)} async-done(((f32[4,832,256]{2,1,0:T(8,128)}), f32[1,832,256]{2,1,0:T(8,128)}) %reduce-scatter.8.cloned.1.call-update) | async-done | bytes 851984 | tf_op jit(solution)/shard_map/reduce_scatter | solution.py:40
  107.0 97.9 %reduce-scatter.6.cloned.1.call-done = f32[1,832,832]{2,1,0:T(8,128)} async-done(((f32[4,832,832]{2,1,0:T(8,128)}), f32[1,832,832]{2,1,0:T(8,128)}) %reduce-scatter.6.cloned.1.call-update) | async-done | bytes 2768912 | tf_op jit(solution)/shard_map/reduce_scatter | solution.py:38
  205.0 154.2 %all-reduce.10.cloned.1.call-done = (f32[832,256]{1,0:T(8,128)}, f32[832,832]{1,0:T(8,128)}, f32[256,256]{0,1:T(8,128)}) async-done(((f32[832,256]{1,0:T(8,128)}, f32[832,832]{1,0:T(8,128)}, f32[256,256]{0,1:T(8,128)}), (f32[832,256]{1,0:T(8,128)}, f32[832,832]{1,0:T(8,128)}, f32[256,256]{0,1:T(8,128)})) %all-reduce.10.cloned.1.call-update) | async-done | bytes 3883024 | tf_op jit(solution)/shard_map/psum | solution.py:43
  360.2 106.4 %all-reduce.12.cloned.1.call-done = (f32[832,256]{1,0:T(8,128)}, f32[832,832]{1,0:T(8,128)}, f32[256,256]{0,1:T(8,128)}) async-done(((f32[832,256]{1,0:T(8,128)}, f32[832,832]{1,0:T(8,128)}, f32[256,256]{0,1:T(8,128)}), (f32[832,256]{1,0:T(8,128)}, f32[832,832]{1,0:T(8,128)}, f32[256,256]{0,1:T(8,128)})) %all-reduce.12.cloned.1.call-update) | async-done | bytes 3883024 | tf_op jit(solution)/shard_map/psum | solution.py:42
  468.9 11.7 %cholesky.237 = f32[128,128]{1,0:T(8,128)S(1)} custom-call(f32[128,128]{1,0:T(8,128)S(1)} %cholesky.611), custom_call_target="Cholesky" | custom-call | tf_op jit(solution)/shard_map/jit(cholesky)/cholesky | solution.py:49
  480.6 9.8 %custom-call.76 = f32[1,128,128]{1,2,0:T(8,128)S(1)} custom-call(f32[1,128,128]{2,1,0:T(8,128)S(1)} %get-tuple-element.62), custom_call_target="InvertDiagBlocksLowerTriangular" | custom-call | tf_op jit(solution)/shard_map/jit(cholesky)/cholesky | solution.py:49
  490.9 11.7 %cholesky.256 = f32[128,128]{1,0:T(8,128)S(1)} custom-call(f32[128,128]{1,0:T(8,128)S(1)} %convolution_subtract_fusion.19), custom_call_target="Cholesky" | custom-call | tf_op jit(solution)/shard_map/jit(cholesky)/cholesky | solution.py:49
  504.9 4.6 copy.11
  513.4 11.7 %cholesky.273 = f32[128,128]{1,0:T(8,128)S(1)} custom-call(f32[128,128]{1,0:T(8,128)S(1)} %cholesky.614), custom_call_target="Cholesky" | custom-call | tf_op jit(solution)/shard_map/jit(cholesky)/cholesky | solution.py:48
  530.5 5.7 while.2
  536.2 21.2 %custom-call.77 = f32[2,128,128]{1,2,0:T(8,128)} custom-call(f32[2,128,128]{2,1,0:T(8,128)} %get-tuple-element.12), custom_call_target="InvertDiagBlocksLowerTriangular" | custom-call | tf_op jit(solution)/shard_map/jit(_cho_solve)/triangular_solve | solution.py:51
  557.4 9.8 %custom-call.78 = f32[1,128,128]{1,2,0:T(8,128)S(1)} custom-call(f32[1,128,128]{2,1,0:T(8,128)S(1)} %get-tuple-element.79), custom_call_target="InvertDiagBlocksLowerTriangular" | custom-call | tf_op jit(solution)/shard_map/jit(cholesky)/cholesky | solution.py:48
  570.8 11.7 %cholesky.496 = f32[128,128]{1,0:T(8,128)S(1)} custom-call(f32[128,128]{1,0:T(8,128)S(1)} %cholesky.618), custom_call_target="Cholesky" | custom-call | tf_op jit(solution)/shard_map/jit(cholesky)/cholesky | solution.py:48
  582.6 9.8 %custom-call.79 = f32[1,128,128]{1,2,0:T(8,128)S(1)} custom-call(f32[1,128,128]{2,1,0:T(8,128)S(1)} %get-tuple-element.76), custom_call_target="InvertDiagBlocksLowerTriangular" | custom-call | tf_op jit(solution)/shard_map/jit(cholesky)/cholesky | solution.py:48
  596.1 12.1 %cholesky.517 = f32[128,128]{1,0:T(8,128)S(1)} custom-call(f32[128,128]{1,0:T(8,128)S(1)} %cholesky.623), custom_call_target="Cholesky" | custom-call | tf_op jit(solution)/shard_map/jit(cholesky)/cholesky | solution.py:48
  608.9 9.8 %custom-call.80 = f32[1,128,128]{1,2,0:T(8,128)S(1)} custom-call(f32[1,128,128]{2,1,0:T(8,128)S(1)} %get-tuple-element.73), custom_call_target="InvertDiagBlocksLowerTriangular" | custom-call | tf_op jit(solution)/shard_map/jit(cholesky)/cholesky | solution.py:48
  622.3 11.7 %cholesky.536 = f32[128,128]{1,0:T(8,128)S(1)} custom-call(f32[128,128]{1,0:T(8,128)S(1)} %cholesky.628), custom_call_target="Cholesky" | custom-call | tf_op jit(solution)/shard_map/jit(cholesky)/cholesky | solution.py:48
  634.8 9.8 %custom-call.81 = f32[1,128,128]{1,2,0:T(8,128)S(1)} custom-call(f32[1,128,128]{2,1,0:T(8,128)S(1)} %get-tuple-element.70), custom_call_target="InvertDiagBlocksLowerTriangular" | custom-call | tf_op jit(solution)/shard_map/jit(cholesky)/cholesky | solution.py:48
  647.5 11.9 %cholesky.555 = f32[128,128]{1,0:T(8,128)S(1)} custom-call(f32[128,128]{1,0:T(8,128)S(1)} %cholesky.633), custom_call_target="Cholesky" | custom-call | tf_op jit(solution)/shard_map/jit(cholesky)/cholesky | solution.py:48
  660.1 9.8 %custom-call.82 = f32[1,128,128]{1,2,0:T(8,128)S(1)} custom-call(f32[1,128,128]{2,1,0:T(8,128)S(1)} %get-tuple-element.67), custom_call_target="InvertDiagBlocksLowerTriangular" | custom-call | tf_op jit(solution)/shard_map/jit(cholesky)/cholesky | solution.py:48
  671.6 11.7 %cholesky.575 = f32[128,128]{1,0:T(8,128)S(1)} custom-call(f32[128,128]{1,0:T(8,128)S(1)} %cholesky.638), custom_call_target="Cholesky" | custom-call | tf_op jit(solution)/shard_map/jit(cholesky)/cholesky | solution.py:48
  684.1 9.8 %custom-call.83 = f32[1,128,128]{1,2,0:T(8,128)S(1)} custom-call(f32[1,128,128]{2,1,0:T(8,128)S(1)} %get-tuple-element.64), custom_call_target="InvertDiagBlocksLowerTriangular" | custom-call | tf_op jit(solution)/shard_map/jit(cholesky)/cholesky | solution.py:48
  695.2 5.8 cholesky.596
  708.8 21.3 %while.3 = (s32[]{:T(128)}, f32[832,832]{1,0:T(8,128)}, s32[6,2]{0,1:T(2,128)S(1)}, f32[6,128,128]{2,1,0:T(8,128)}, s32[]{:T(128)}) while((s32[]{:T(128)}, f32[832,832]{1,0:T(8,128)}, s32[6,2]{0,1:T(2,128)S(1)}, f32[6,128,128]{2,1,0:T(8,128)}, s32[]{:T(128)}) %tuple.83), condition=%wide.while_cond.1, body=%wide.while_body.1.sunk | while | flops 2 | bytes 132705 | solution.py:50
  732.1 70.4 %custom-call.84 = f32[7,128,128]{1,2,0:T(8,128)} custom-call(f32[7,128,128]{2,1,0:T(8,128)} %pad_maximum_fusion), custom_call_target="InvertDiagBlocksLowerTriangular" | custom-call | tf_op jit(solution)/shard_map/jit(_cho_solve)/triangular_solve | solution.py:50
  823.0 6.4 all-reduce.4
  830.7 19.7 %all-gather.3.cloned.1.call-done = f32[3328,256]{1,0:T(8,128)} async-done(((f32[832,256]{1,0:T(8,128)}), f32[3328,256]{1,0:T(8,128)}) %all-gather.3.cloned.1.call-update) | async-done | bytes 3407888 | tf_op jit(solution)/shard_map/all_gather | solution.py:54
  850.4 3.9 broadcast_multiply_fusion
  (187 shorter events, 87.3 us)
Async XLA Ops:
  6.5 5.9 copy-start.11
  6.5 86.0 %reduce-scatter.4.cloned.1.call-start = ((), (), s32[]{:S(2)}) async-start(), calls=%async_computation.3 | async-start | bytes 1310720 | tf_op jit(solution)/shard_map/reduce_scatter | solution.py:39
  12.4 94.6 %reduce-scatter.8.cloned.1.call-start = ((), (), s32[]{:S(2)}) async-start(), calls=%async_computation.5 | async-start | bytes 4259840 | tf_op jit(solution)/shard_map/reduce_scatter | solution.py:40
  67.3 137.6 %reduce-scatter.6.cloned.1.call-start = ((), (), s32[]{:S(2)}) async-start(), calls=%async_computation.4 | async-start | bytes 14909440 | tf_op jit(solution)/shard_map/reduce_scatter | solution.py:38
  92.5 266.8 %all-reduce.10.cloned.1.call-start = ((), (), s32[]{:S(2)}) async-start(), calls=%async_computation.7 | async-start | bytes 8192000 | tf_op jit(solution)/shard_map/psum | solution.py:43
  205.0 261.6 %all-reduce.12.cloned.1.call-start = ((), (), s32[]{:S(2)}) async-start(), calls=%async_computation.8 | async-start | bytes 8192000 | tf_op jit(solution)/shard_map/psum | solution.py:42
  359.3 491.1 %all-gather.3.cloned.1.call-start = ((), (), s32[]{:S(2)}) async-start(), calls=%async_computation.6 | async-start | bytes 4259840 | tf_op jit(solution)/shard_map/all_gather | solution.py:54
  466.6 36.4 %copy-start = (f32[832,832]{1,0:T(8,128)S(1)}, f32[832,832]{1,0:T(8,128)}, u32[]{:S(2)}) copy-start(f32[832,832]{1,0:T(8,128)} %get-tuple-element.45) | copy-start | bytes 8306692
  511.7 1.6 copy-start.3
  570.1 0.7 copy-start.6
  595.4 0.7 copy-start.7
  621.6 0.7 copy-start.8
  707.0 23.1 %copy-start.10 = (f32[128,64]{1,0:T(8,128)S(1)}, f32[128,64]{1,0:T(8,128)}, u32[]{:S(2)}) copy-start(f32[128,64]{1,0:T(8,128)} %pad_convert_fusion) | copy-start | bytes 98308
  707.2 1.6 copy-start.1
  730.1 74.9 %copy-start.2 = (f32[832,832]{1,0:T(8,128)S(1)}, f32[832,832]{1,0:T(8,128)}, u32[]{:S(2)}) copy-start(f32[832,832]{1,0:T(8,128)} %get-tuple-element.207) | copy-start | bytes 8306692
  802.5 4.2 copy-start.5
  813.3 2.3 copy-start.9
  817.2 2.9 copy-start.12
  817.2 3.5 copy-start.4
Sparse Core Ops, SparseCore 0:
  12.5 27.5 reduce-scatter.3
  67.5 39.5 reduce-scatter.7
  109.7 95.2 reduce-scatter.5
  207.4 151.8 all-reduce.9
  361.7 104.8 all-reduce.11
  820.3 30.0 all-gather.2
